TPU v7x, 128 devices: a whole 4x4x4 slice. The times are simulated.
128 devices in a mesh: rows: 16 (over x, z), cols: 8 (over y, core).
Axes of the slice: x: 4, y: 4, z: 4, core: 2. Of those that a mesh axis runs over, the one named last changes fastest.
Arguments:
- bag_index: int32 [2048, 128], P(('rows', 'cols')), may hold values from 0 to 1048575, as said below
- bag_length: int32 [2048, 4], P(('rows', 'cols')), may hold values from 1 to 32
- emb_tables: float32 [4, 1048576, 128], P(None, ('rows', 'cols')), may hold values from -0.6 to 0.6
- dense_feats: float32 [2048, 128], P(('rows', 'cols')), may hold values from -6 to 6
- w_dense: float32 [128, 1024], replicated, may hold values from -0.5 to 0.5
- w_pair: float32 [10, 1024], replicated, may hold values from -0.5 to 0.5
- top_bias: float32 [1024], replicated, may hold values from -3 to 3
Outputs:
- pooled: float32 [2048, 4, 128], P(('rows', 'cols'))
- top_hidden: float32 [2048, 1024], P(('rows', 'cols'))
Inputs may be any that keep to these rules, and one draw needn't show every extreme that they name: `bag_length`: slots at or past a bag's length are ignored, whatever they hold. `bag_index`: device d holds rows d * 8192 to (d + 1) * 8192 - 1 of every table; among the 2048 slots (live or not) of the samples of one device, at most 32 hold rows of any one device, and in every draw some device's rows receive exactly 32 slots from every device.
All inputs are finite; a program needn't handle non-finite values.
Results may differ from a plain program's by a relative error of at most 0.0001.
Values sent between devices are 32-bit elements; how exact they have to be, the bound alone decides.
A program may use at most 128 MiB of HBM per device.

v0:
```python
import jax
import jax.numpy as jnp
from jax import lax
from jax.sharding import PartitionSpec as P

NT = 4
L = 32


def interact(dense_feats, pooled, w_dense, w_pair, top_bias):
    feats = [dense_feats] + [pooled[:, t, :] for t in range(NT)]
    pair_list = []
    for first in range(NT + 1):
        for second in range(first + 1, NT + 1):
            pair_list.append(jnp.sum(feats[first] * feats[second], axis=-1))
    pair_dots = jnp.stack(pair_list, axis=1)
    hidden = jnp.dot(
        dense_feats, w_dense, precision=lax.Precision.HIGHEST, preferred_element_type=jnp.float32
    )
    hidden = hidden + jnp.dot(
        pair_dots, w_pair, precision=lax.Precision.HIGHEST, preferred_element_type=jnp.float32
    )
    return jnp.maximum(hidden + top_bias, 0.0)


def shards(bag_index, bag_length, emb_tables, dense_feats, w_dense, w_pair, top_bias):
    samples = bag_index.shape[0]
    local_rows = emb_tables.shape[1]
    width = emb_tables.shape[2]
    position = jnp.arange(L, dtype=jnp.int32)
    devices = lax.axis_size("rows") * lax.axis_size("cols")
    slots = samples * NT * L
    capacity = 2 * slots // devices
    flat_ids = bag_index.reshape(slots)
    target = flat_ids // local_rows
    slot_iota = jnp.arange(slots, dtype=jnp.int32)
    table_of = slot_iota % (NT * L) // L
    code = table_of * local_rows + flat_ids - target * local_rows
    earlier = (slot_iota[None, :] < slot_iota[:, None]) & (target[None, :] == target[:, None])
    rank = jnp.sum(earlier.astype(jnp.int32), axis=1)
    owner_hot = (target[:, None] == jnp.arange(devices, dtype=jnp.int32)[None, :]).astype(
        jnp.float32
    )
    rank_hot = (rank[:, None] == jnp.arange(capacity, dtype=jnp.int32)[None, :]).astype(jnp.float32)
    weighted = owner_hot * code.astype(jnp.float32)[:, None]
    outbox = jnp.einsum(
        "sd,sc->dc",
        weighted,
        rank_hot,
        precision=lax.Precision.HIGHEST,
        preferred_element_type=jnp.float32,
    )
    outbox = outbox.astype(jnp.int32)
    flat_table = emb_tables.reshape(NT * local_rows, width)
    found = jnp.take(
        flat_table,
        lax.all_to_all(outbox, ("rows", "cols"), split_axis=0, concat_axis=0, tiled=True),
        axis=0,
    )
    fetched = lax.all_to_all(found, ("rows", "cols"), split_axis=0, concat_axis=0, tiled=True)
    place = target * capacity + rank
    selector = (place[:, None] == jnp.arange(devices * capacity, dtype=jnp.int32)[None, :]).astype(
        jnp.float32
    )
    picked = jnp.dot(
        selector,
        fetched.reshape(devices * capacity, width),
        precision=lax.Precision.HIGHEST,
        preferred_element_type=jnp.float32,
    )
    picked = picked.reshape(samples, NT, L, width)
    live = position[None, None, :] < bag_length[:, :, None]
    pooled = jnp.sum(jnp.where(live[:, :, :, None], picked, 0.0), axis=2)
    return (pooled, interact(dense_feats, pooled, w_dense, w_pair, top_bias))


def solution(mesh):
    in_specs = (
        P(("rows", "cols"), None),
        P(("rows", "cols"), None),
        P(None, ("rows", "cols"), None),
        P(("rows", "cols"), None),
        P(),
        P(),
        P(),
    )
    out_specs = (P(("rows", "cols"), None, None), P(("rows", "cols"), None))
    return jax.shard_map(shards, mesh=mesh, in_specs=in_specs, out_specs=out_specs, check_vma=False)
```

profile of v0, /device:TPU:0, one launch (start us, length us, event | category | flops | bytes accessed | tf_op | source)
XLA Modules:
  0.0 99.2 jit_solution(9859492654781708526)
XLA Ops:
  0.6 0.0 copy-start
  0.6 0.8 fusion.28
  1.4 4.6 %convert_reduce_fusion = s32[2048]{0:T(1024)S(1)} fusion(s32[2048]{0:T(1024)S(1)} %get-tuple-element.17), kind=kLoop, calls=%fused_computation.5 | loop fusion | flops 20969472 | bytes 16384 | tf_op jit(solution)/shard_map/reduce_sum | solution.py:40
  6.0 1.9 %fusion.13 = s32[128,1,32]{0,2,1:T(8,128)S(1)} fusion(s32[2048]{0:T(1024)S(1)} %convert_reduce_fusion, f32[2048]{0:T(1024)S(1)} %get-tuple-element.16, s32[2048]{0:T(1024)S(1)} %get-tuple-element.17), kind=kOutput, calls=%fused_computation.14 | convolution fusion | flops 101257216 | bytes 40960 | tf_op jit(solution)/shard_map/sd,sc->dc/dot_general | solution.py:46
  7.9 0.1 copy.26
  8.0 20.3 %all_to_all.20 = s32[128,1,32]{2,1,0:T(1,128)S(1)} all-to-all(s32[128,1,32]{2,1,0:T(1,128)S(1)} %copy.26), channel_id=1, replica_groups=mesh['rows'=16,'cols'=8] {'rows','cols'}, dimensions={0} | all-to-all | bytes 32768 | tf_op jit(solution)/shard_map/all_to_all | solution.py:57
  28.3 0.1 reshape.198
  28.4 16.5 %gather_fusion = f32[4096,128]{1,0:T(8,128)S(1)} fusion(f32[32768,128]{1,0:T(8,128)} %bitcast.64, s32[4096]{0:T(1024)S(1)} %broadcast_clamp_fusion), kind=kCustom, calls=%fused_computation | custom fusion | bytes 4210688 | tf_op jit(solution)/shard_map/jit(_take)/gather | solution.py:55
  45.0 0.0 copy-start.3
  45.0 0.0 copy-start.6
  45.0 0.0 copy-start.2
  45.0 2.4 %broadcast_select_fusion = f32[128,32,128]{2,1,0:T(8,128)} fusion(f32[128,32,128]{2,1,0:T(8,128)S(1)} %bitcast.65, pred[128,32]{1,0:T(8,128)(4,1)S(1)} %compare_and_fusion), kind=kLoop, calls=%fused_computation.15 | loop fusion | flops 524288 | bytes 4198400 | tf_op jit(solution)/shard_map/jit(_take)/select_n | solution.py:55
  47.4 5.0 %all-to-all-start.1 = ((f32[128,32,128]{2,1,0:T(8,128)}), f32[128,32,128]{2,1,0:T(8,128)S(1)}, u32[]{:S(2)}, u32[]{:S(2)}) async-start(f32[128,32,128]{2,1,0:T(8,128)} %broadcast_select_fusion), calls=%async_computation.1 | async-start | bytes 4194304 | tf_op jit(solution)/shard_map/all_to_all | solution.py:60
  52.4 0.1 reduce_sum.111
  52.5 0.0 copy-done.3
  52.5 0.1 reshape.192
  52.6 0.0 copy-done.6
  52.6 0.1 copy.25
  52.7 0.1 iota_compare_fusion.6
  52.9 0.0 copy-done
  52.9 0.0 copy-done.2
  52.9 0.4 fusion.38
  53.2 29.4 %all-to-all-done.1 = f32[128,32,128]{2,1,0:T(8,128)S(1)} async-done(((f32[128,32,128]{2,1,0:T(8,128)}), f32[128,32,128]{2,1,0:T(8,128)S(1)}, u32[]{:S(2)}, u32[]{:S(2)}) %all-to-all-start.1) | async-done | bytes 2097184 | tf_op jit(solution)/shard_map/all_to_all | solution.py:60
  82.6 0.0 copy-start.1
  82.6 0.0 copy-start.5
  82.6 15.3 %fusion.8 = f32[16,4,128]{2,1,0:T(4,128)S(1)} fusion(f32[4096,128,1,1]{1,0,3,2:T(8,128)S(1)} %bitcast.66, s32[16,4,32]{2,1,0:T(4,128)S(1)} %fusion.21, pred[16,4,32]{2,1,0:T(4,128)(4,1)S(1)} %iota_compare_fusion.6), kind=kOutput, calls=%fused_computation.9 | convolution fusion | flops 12893806592 | bytes 2140160 | tf_op jit(solution)/shard_map/dot_general | solution.py:65
  98.0 0.0 copy-start.4
  98.0 0.3 multiply_reduce_fusion
  98.3 0.0 copy-done.1
  98.3 0.0 copy-done.5
  98.3 0.9 fusion.12
  99.2 0.0 copy-done.4
  (6 shorter events, 0.2 us)
Async XLA Ops:
  0.6 52.2 %copy-start = (f32[128,1024]{1,0:T(8,128)S(1)}, f32[128,1024]{1,0:T(8,128)}, u32[]{:S(2)}) copy-start(f32[128,1024]{1,0:T(8,128)} %param.11) | copy-start | bytes 1572868
  45.0 7.6 %copy-start.3 = (s32[16,128]{1,0:T(8,128)S(1)}, s32[16,128]{1,0:T(8,128)}, u32[]{:S(2)}) copy-start(s32[16,128]{1,0:T(8,128)} %param.7) | copy-start | bytes 24580
  45.0 7.6 %copy-start.6 = (s32[16,4]{0,1:T(4,128)S(1)}, s32[16,4]{0,1:T(4,128)}, u32[]{:S(2)}) copy-start(s32[16,4]{0,1:T(4,128)} %param.8) | copy-start | bytes 772
  45.0 7.9 %copy-start.2 = (f32[16,128]{1,0:T(8,128)S(1)}, f32[16,128]{1,0:T(8,128)}, u32[]{:S(2)}) copy-start(f32[16,128]{1,0:T(8,128)} %param.10) | copy-start | bytes 24580
  47.4 35.2 %all-to-all-start.1 = ((f32[128,32,128]{2,1,0:T(8,128)}), f32[128,32,128]{2,1,0:T(8,128)S(1)}, u32[]{:S(2)}, u32[]{:S(2)}) async-start(f32[128,32,128]{2,1,0:T(8,128)} %broadcast_select_fusion), calls=%async_computation.1 | async-start | bytes 4194304 | tf_op jit(solution)/shard_map/all_to_all | solution.py:60
  82.6 15.7 %copy-start.1 = (f32[10,1024]{1,0:T(8,128)S(1)}, f32[10,1024]{1,0:T(8,128)}, u32[]{:S(2)}) copy-start(f32[10,1024]{1,0:T(8,128)} %param.12) | copy-start | bytes 122884
  82.6 15.7 %copy-start.5 = (f32[1024]{0:T(1024)S(1)}, f32[1024]{0:T(1024)}, u32[]{:S(2)}) copy-start(f32[1024]{0:T(1024)} %param.13) | copy-start | bytes 12292
  98.0 1.3 %copy-start.4 = (f32[16,4,128]{2,1,0:T(4,128)}, f32[16,4,128]{2,1,0:T(4,128)S(1)}, u32[]{:S(2)}) copy-start(f32[16,4,128]{2,1,0:T(4,128)S(1)} %fusion.8) | copy-start | bytes 98308
where the time goes:
time: 99.6 us; the launch traced here: 99.2 us
  waiting for transfers between devices  29.4 us (30%)
  blocking collectives  20.3 us (20%)
  matrix products  18.4 us (18%)
  local copies, waits for them, and re-layouts  17.1 us (17%)
  other arithmetic  8.24 us (8%)
  starting transfers between devices  4.99 us (5%)
    all_to_all x1, waiting for transfers between devices, shards(): lax.all_to_all(found, ('rows', 'cols'), split_axis=0, concat_axis=0, tile...  29.4 us
    all_to_all x1, blocking collectives, shards(): lax.all_to_all(outbox, ('rows', 'cols'), split_axis=0, concat_axis=0, til...  20.3 us
    gather x1, local copies, waits for them, and re-layouts, shards(): jnp.take(flat_table, lax.all_to_all(outbox, ('rows', 'cols'), split_axis=...  16.5 us
    dot_general x1, matrix products, shards(): jnp.dot(selector, fetched.reshape(devices * capacity, width), precision=l...  15.3 us
    all_to_all x1, starting transfers between devices, shards(): lax.all_to_all(found, ('rows', 'cols'), split_axis=0, concat_axis=0, tile...  4.99 us
    reduce_sum x1, other arithmetic, shards(): rank = jnp.sum(earlier.astype(jnp.int32), axis=1)  4.6 us
    select_n x2, other arithmetic, shards(): jnp.take(flat_table, lax.all_to_all(outbox, ('rows', 'cols'), split_axis=...  2.44 us
  transfers between devices with their start and end apart: 1, of which 1 were waited for; matrix products, arithmetic and copies ran while one was open for 1% of the time, Pallas kernels for 0%

commit v1 on v0

v1 whole, which is shorter than its diff:
```python
import functools

import jax
import jax.numpy as jnp
from jax import lax
from jax.experimental import pallas as pl
from jax.experimental.pallas import tpu as pltpu
from jax.sharding import PartitionSpec as P

NT = 4
L = 32
E = 128
NDEV = 128
CAP = 32
BAGS = 64
MIX, UNMIX = 37, 45
CHUNKS = 4
TAB_PARTS = 8
MESH = pl.DeviceIdType.MESH
F32, BF16, I32 = jnp.float32, jnp.bfloat16, jnp.int32
NT_DIMS = (((1,), (1,)), ((), ()))
TN_DIMS = (((0,), (0,)), ((), ()))
NN_DIMS = (((1,), (0,)), ((), ()))


def dot(a, b, dims=NN_DIMS):
    return lax.dot_general(a, b, dims, preferred_element_type=F32)


def split2(v):
    hi = v.astype(BF16)
    return hi, (v - hi.astype(F32)).astype(BF16)


def position():
    r, c = lax.axis_index("rows"), lax.axis_index("cols")
    return lax.div(r, 4), lax.rem(r, 4), lax.div(c, 2), lax.rem(c, 2)


def shifted(me, step, sign):
    s = lax.rem(step * MIX, NDEV)
    digits = (lax.div(s, 32), lax.rem(lax.div(s, 8), 4), lax.rem(lax.div(s, 2), 4), lax.rem(s, 2))
    sizes = (4, 4, 4, 2)
    x, z, y, c = [lax.rem(m + n + sign * d, n) for m, d, n in zip(me, digits, sizes)]
    return x * 4 + z, y * 2 + c


def kernel(idx_hbm, len_hbm, tab_hbm, dense_hbm, wd_hbm, wp_hbm, bias_hbm, pooled_out, hidden_out,
           idx_ref, len_ref, tab, dense_ref, wd, wp, bias, ohs, vhi, vlo, vbag, outbox, inbox, checked, ids, gath, fetched, wsel,
           load_sem, tab_sem, ids_send, ids_recv, smem_sem, row_send, row_recv):
    me = position()
    loads = [pltpu.make_async_copy(s, d, load_sem.at[n]) for n, (s, d) in
             enumerate(((idx_hbm, idx_ref), (len_hbm, len_ref), (dense_hbm, dense_ref), (wd_hbm, wd), (wp_hbm, wp),
                        (bias_hbm, bias)))]
    part = tab.shape[0] // TAB_PARTS
    tab_loads = [pltpu.make_async_copy(tab_hbm.at[pl.ds(n * part, part)], tab.at[pl.ds(n * part, part)], tab_sem.at[n])
                 for n in range(TAB_PARTS)]

    for cp in loads[:2] + tab_loads + loads[2:]:
        cp.start()
    barrier = pltpu.get_barrier_semaphore()

    @pl.loop(1, NDEV)
    def _(step):
        pl.semaphore_signal(barrier, inc=1, device_id=shifted(me, step, 1), device_id_type=MESH)


    for cp in loads[:2]:
        cp.wait()
    idx = idx_ref[...]
    local_rows = tab.shape[0] // NT
    lane = lax.broadcasted_iota(I32, (16, NDEV), 1)
    table_of = lane // L
    of_table = (lax.broadcasted_iota(I32, (NT, NDEV), 1) // L == lax.broadcasted_iota(I32, (NT, NDEV), 0)).astype(F32)
    limit = dot(len_ref[...].astype(F32), of_table, TN_DIMS).astype(I32)
    live = lane % L < limit
    owner = idx // local_rows
    code = table_of * local_rows + idx % local_rows
    ox, oz, oy, oc = owner // 32, owner // 8 % 4, owner // 2 % 4, owner % 2
    x, z, y, c = me
    s = (ox - x + 4) % 4 * 32 + (oz - z + 4) % 4 * 8 + (oy - y + 4) % 4 * 2 + (oc - c + 2) % 2
    rel = jnp.where(live, s * UNMIX % NDEV, -1)
    bag = lax.broadcasted_iota(I32, (16, NDEV), 0) + 16 * table_of + 1
    sub = lax.broadcasted_iota(I32, (NDEV, NDEV), 0)
    lan = lax.broadcasted_iota(I32, (NDEV, NDEV), 1)
    before = jnp.concatenate([(sub < lan).astype(F32), jnp.ones((NDEV, NDEV), F32)], axis=1).astype(BF16)
    code_hi, code_lo, bag = (code // 256).astype(F32), (code % 256).astype(F32), bag.astype(F32)
    carry = jnp.zeros((NDEV, NDEV), F32)
    for r in range(16):
        oh = (sub == rel[r:r + 1, :]).astype(F32)
        ohb = oh.astype(BF16)
        counts = dot(ohb, before)
        rank = jnp.sum(oh * (counts[:, :NDEV] + carry), axis=0, keepdims=True).astype(I32)
        carry = carry + counts[:, NDEV:]
        cols = slice(r * NDEV, (r + 1) * NDEV)
        here = sub[:CAP] == rank
        ohs[:, cols] = ohb
        vhi[:, cols] = jnp.where(here, code_hi[r:r + 1], 0.0).astype(BF16)
        vlo[:, cols] = jnp.where(here, code_lo[r:r + 1], 0.0).astype(BF16)
        vbag[:, cols] = jnp.where(sub % CAP == rank, bag[r:r + 1], 0.0).astype(BF16)
    all_oh = ohs[...]
    box = dot(all_oh, vhi[...], NT_DIMS) * 256.0 + dot(all_oh, vlo[...], NT_DIMS)
    outbox[...] = box.astype(I32).reshape(NDEV, 1, CAP)
    inbox[0] = outbox[0]

    pl.semaphore_wait(barrier, NDEV - 1)

    def ids_copy(step):
        return pltpu.make_async_remote_copy(
            src_ref=outbox.at[step], dst_ref=inbox.at[step], send_sem=ids_send, recv_sem=ids_recv,
            device_id=shifted(me, step, 1), device_id_type=MESH)

    @pl.loop(1, NDEV)
    def _(step):
        ids_copy(step).start()

    bags = dot(all_oh, vbag[...], NT_DIMS)
    bags = jnp.where(lan // CAP == sub % 4, bags, 0.0).astype(BF16)
    groups = NDEV // 4
    gather4 = (lax.broadcasted_iota(I32, (groups, NDEV), 1) // 4
               == lax.broadcasted_iota(I32, (groups, NDEV), 0)).astype(F32).astype(BF16)
    group_bags = dot(gather4, bags).astype(I32)
    want = lax.broadcasted_iota(I32, (BAGS, NDEV), 0) + 1
    for g in range(groups):
        wsel[:, g * NDEV:(g + 1) * NDEV] = (want == group_bags[g:g + 1, :]).astype(F32).astype(BF16)
    for cp in loads[2:]:
        cp.wait()
    dense = dense_ref[...]
    hidden = lax.dot_general(dense, wd[...], NN_DIMS, precision=lax.Precision.HIGHEST,
                             preferred_element_type=F32) + bias[...]
    for cp in tab_loads:
        cp.wait()

    whole = pltpu.make_async_remote_copy(
        src_ref=outbox.at[pl.ds(1, NDEV - 1)], dst_ref=inbox.at[pl.ds(1, NDEV - 1)], send_sem=ids_send,
        recv_sem=ids_recv, device_id=shifted(me, 1, 1), device_id_type=MESH)
    whole.wait_recv()
    checked[...] = jnp.clip(inbox[...], 0, tab.shape[0] - 1)
    to_smem = pltpu.make_async_copy(checked, ids, smem_sem)
    to_smem.start()
    to_smem.wait()

    per = NDEV // CHUNKS

    def gather(step, dst):
        for j in range(CAP):
            dst[step, j:j + 1, :] = tab[pl.ds(ids[step, 0, j], 1), :]

    def row_copy(step, chunk):
        return pltpu.make_async_remote_copy(
            src_ref=gath.at[step], dst_ref=fetched.at[step], send_sem=row_send.at[0], recv_sem=row_recv.at[chunk],
            device_id=shifted(me, step, -1), device_id_type=MESH)

    gather(0, fetched)
    for chunk in range(CHUNKS):
        @pl.loop(1 if chunk == 0 else chunk * per, (chunk + 1) * per)
        def _(step):
            gather(step, gath)
            row_copy(step, chunk).start()

    total = jnp.zeros((BAGS, E), F32)
    for chunk in range(CHUNKS):
        first = 1 if chunk == 0 else chunk * per
        span = pl.ds(first, (chunk + 1) * per - first)
        pltpu.make_async_remote_copy(
            src_ref=gath.at[span], dst_ref=fetched.at[span], send_sem=row_send.at[0], recv_sem=row_recv.at[chunk],
            device_id=shifted(me, 1, 1), device_id_type=MESH).wait_recv()
        got = fetched[chunk * per:(chunk + 1) * per].reshape(per * CAP, E)
        hi, lo = split2(got)
        w = wsel[:, chunk * per * CAP:(chunk + 1) * per * CAP]
        total = total + (dot(w, hi) + dot(w, lo))

    feats = [dense] + [total[t * 16:(t + 1) * 16] for t in range(NT)]
    for t in range(NT):
        pooled_out[:, t, :] = feats[t + 1]
    k = 0
    for a in range(NT + 1):
        for b in range(a + 1, NT + 1):
            d = jnp.sum(feats[a] * feats[b], axis=-1, keepdims=True)
            hidden = hidden + d * wp[k:k + 1, :]
            k += 1
    hidden_out[...] = jnp.maximum(hidden, 0.0)

    whole.wait_send()
    everything = pl.ds(1, NDEV - 1)
    pltpu.make_async_remote_copy(
        src_ref=gath.at[everything], dst_ref=fetched.at[everything], send_sem=row_send.at[0], recv_sem=row_recv.at[0],
        device_id=shifted(me, 1, 1), device_id_type=MESH).wait_send()


def shards(bag_index, bag_length, emb_tables, dense_feats, w_dense, w_pair, top_bias):
    rows = NT * emb_tables.shape[1]
    hidden = w_dense.shape[1]
    slots = 16 * NDEV
    vmem, hbm = pl.BlockSpec(memory_space=pltpu.VMEM), pl.BlockSpec(memory_space=pltpu.HBM)
    return pl.pallas_call(
        kernel,
        out_shape=(jax.ShapeDtypeStruct((16, NT, E), F32), jax.ShapeDtypeStruct((16, hidden), F32)),
        in_specs=[hbm] * 7,
        out_specs=(vmem, vmem),
        scratch_shapes=[
            pltpu.VMEM((16, NDEV), I32),
            pltpu.VMEM((NT, 16), I32),
            pltpu.VMEM((rows, E), F32),
            pltpu.VMEM((16, E), F32),
            pltpu.VMEM(w_dense.shape, F32),
            pltpu.VMEM(w_pair.shape, F32),
            pltpu.VMEM((1, hidden), F32),
            pltpu.VMEM((NDEV, slots), BF16),
            pltpu.VMEM((CAP, slots), BF16),
            pltpu.VMEM((CAP, slots), BF16),
            pltpu.VMEM((NDEV, slots), BF16),
            pltpu.VMEM((NDEV, 1, CAP), I32),
            pltpu.VMEM((NDEV, 1, CAP), I32),
            pltpu.VMEM((NDEV, 1, CAP), I32),
            pltpu.SMEM((NDEV, 1, CAP), I32),
            pltpu.VMEM((NDEV, CAP, E), F32),
            pltpu.VMEM((NDEV, CAP, E), F32),
            pltpu.VMEM((BAGS, NDEV * CAP), BF16),
            pltpu.SemaphoreType.DMA((6,)),
            pltpu.SemaphoreType.DMA((TAB_PARTS,)),
            pltpu.SemaphoreType.DMA,
            pltpu.SemaphoreType.DMA,
            pltpu.SemaphoreType.DMA,
            pltpu.SemaphoreType.DMA((1,)),
            pltpu.SemaphoreType.DMA((CHUNKS,)),
        ],
        compiler_params=pltpu.CompilerParams(
            collective_id=0, has_side_effects=True, vmem_limit_bytes=60 * 1024 * 1024),
    )(bag_index, bag_length.T, emb_tables.reshape(rows, E), dense_feats, w_dense, w_pair, top_bias.reshape(1, hidden))


def solution(mesh):
    samples = P(("rows", "cols"), None)
    in_specs = (samples, samples, P(None, ("rows", "cols"), None), samples, P(), P(), P())
    out_specs = (P(("rows", "cols"), None, None), samples)
    return jax.shard_map(shards, mesh=mesh, in_specs=in_specs, out_specs=out_specs, check_vma=False)
```

time: 99.6 us -> 54.6 us (0.55)
  the two profiles are of different devices: /device:TPU:0 before, /device:TPU:1 now
where the time goes in v1:
time: 54.6 us; the launch traced here: 54.4 us
  Pallas kernels  50.9 us (93%)
  local copies, waits for them, and re-layouts  2.85 us (5%)
  between operations  0.64 us (1%)
    pallas_call x1, Pallas kernels, shards(): pl.pallas_call(kernel, out_shape=(jax.ShapeDtypeStruct((16, NT, E), F32),...  50.9 us
    unnamed x2, local copies, waits for them, and re-layouts  2.85 us

profile of v1, /device:TPU:1, one launch (start us, length us, event | category | flops | bytes accessed | tf_op | source)
XLA Modules:
  0.0 54.4 jit_solution(13488515107256039376)
XLA Ops:
  0.6 50.9 %shard_map.86 = (f32[16,4,128]{2,1,0:T(4,128)}, f32[16,1024]{1,0:T(8,128)}) custom-call(s32[16,128]{1,0:T(8,128)} %idx_hbm.1, s32[4,16]{1,0:T(4,128)} %bitcast.5, f32[32768,128]{1,0:T(8,128)} %bitcast.3, f32[16,128]{1,0:T(8,128)} %dense_hbm.1, f32[128,1024]{1,0:T(8,128)} %wd_hbm.1, f32[10,1024]{1,0:T(8,128)} %wp_hbm.1, f32[1,1024]{1,0:T(1,128)} %bitcast.4), custom_call_target="tpu_custom_call" | custom-call | tf_op jit(solution)/shard_map/pallas_call | solution.py:196
  51.6 1.4 %copy.11 = f32[16,4,128]{2,1,0:T(4,128)} copy(f32[16,4,128]{2,1,0:T(4,128)} %get-tuple-element.4) | data formatting | bytes 65536
  52.9 1.5 %copy.12 = f32[16,1024]{1,0:T(8,128)} copy(f32[16,1024]{1,0:T(8,128)} %get-tuple-element.5) | data formatting | bytes 131072

commit v2 on v1

v2 whole, which is shorter than its diff:
```python
import functools

import jax
import jax.numpy as jnp
from jax import lax
from jax.experimental import pallas as pl
from jax.experimental.pallas import tpu as pltpu
from jax.sharding import PartitionSpec as P

NT = 4
L = 32
E = 128
NDEV = 128
CAP = 32
BAGS = 64
TAB_PARTS = 8
MESH = pl.DeviceIdType.MESH
F32, BF16, I32 = jnp.float32, jnp.bfloat16, jnp.int32
NT_DIMS = (((1,), (1,)), ((), ()))
TN_DIMS = (((0,), (0,)), ((), ()))
NN_DIMS = (((1,), (0,)), ((), ()))


def dot(a, b, dims=NN_DIMS):
    return lax.dot_general(a, b, dims, preferred_element_type=F32)


def split2(v):
    hi = v.astype(BF16)
    return hi, (v - hi.astype(F32)).astype(BF16)


def position():
    r, c = lax.axis_index("rows"), lax.axis_index("cols")
    return lax.div(r, 4), lax.rem(r, 4), lax.div(c, 2), lax.rem(c, 2)


def around(at, n, sign=1):
    return [lax.rem(at + n + sign * d, n) for d in range(n)]


def kernel(idx_hbm, len_hbm, tab_hbm, dense_hbm, wd_hbm, wp_hbm, bias_hbm, pooled_out, hidden_out,
           idx_ref, len_ref, tab, dense_ref, wd, wp, bias, ohs, vhi, vlo, vbag, outbox, passing, inbox, checked, ids, mybags, linebags, stage, agg, sums, parts,
           load_sem, tab_sem, ids_send, ids_recv, smem_sem, bag_send, bag_recv, row_send, row_recv, sum_send, sum_recv):
    me = position()
    loads = [pltpu.make_async_copy(s, d, load_sem.at[n]) for n, (s, d) in
             enumerate(((idx_hbm, idx_ref), (len_hbm, len_ref), (dense_hbm, dense_ref), (wd_hbm, wd), (wp_hbm, wp),
                        (bias_hbm, bias)))]
    part = tab.shape[0] // TAB_PARTS
    tab_loads = [pltpu.make_async_copy(tab_hbm.at[pl.ds(n * part, part)], tab.at[pl.ds(n * part, part)], tab_sem.at[n])
                 for n in range(TAB_PARTS)]

    for cp in loads[:2] + tab_loads + loads[2:]:
        cp.start()
    barrier = pltpu.get_barrier_semaphore()

    my_row, my_col = lax.axis_index("rows"), lax.axis_index("cols")
    xs, zs, ys, cs = [around(at, n) for at, n in zip(me, (4, 4, 4, 2))]
    line = [(my_row, y * 2 + c) for y in ys for c in cs]
    plane = [(x * 4 + z, my_col) for x in xs for z in zs]
    for peer in plane[1:] + line[1:]:
        pl.semaphore_signal(barrier, inc=1, device_id=peer, device_id_type=MESH)


    for cp in loads[:2]:
        cp.wait()
    idx = idx_ref[...]
    local_rows = tab.shape[0] // NT
    lane = lax.broadcasted_iota(I32, (16, NDEV), 1)
    table_of = lane // L
    of_table = (lax.broadcasted_iota(I32, (NT, NDEV), 1) // L == lax.broadcasted_iota(I32, (NT, NDEV), 0)).astype(F32)
    limit = dot(len_ref[...].astype(F32), of_table, TN_DIMS).astype(I32)
    live = lane % L < limit
    owner = idx // local_rows
    code = table_of * local_rows + idx % local_rows
    ox, oz, oy, oc = owner // 32, owner // 8 % 4, owner // 2 % 4, owner % 2
    x, z, y, c = me
    slot = (oy - y + 4) % 4 * 32 + (oc - c + 2) % 2 * 16 + (ox - x + 4) % 4 * 4 + (oz - z + 4) % 4
    rel = jnp.where(live, slot, -1)
    bag = lax.broadcasted_iota(I32, (16, NDEV), 0) + 16 * table_of + 1
    sub = lax.broadcasted_iota(I32, (NDEV, NDEV), 0)
    lan = lax.broadcasted_iota(I32, (NDEV, NDEV), 1)
    before = jnp.concatenate([(sub < lan).astype(F32), jnp.ones((NDEV, NDEV), F32)], axis=1).astype(BF16)
    code_hi, code_lo, bag = (code // 256).astype(F32), (code % 256).astype(F32), bag.astype(F32)
    carry = jnp.zeros((NDEV, NDEV), F32)
    for r in range(16):
        oh = (sub == rel[r:r + 1, :]).astype(F32)
        ohb = oh.astype(BF16)
        counts = dot(ohb, before)
        rank = jnp.sum(oh * (counts[:, :NDEV] + carry), axis=0, keepdims=True).astype(I32)
        carry = carry + counts[:, NDEV:]
        cols = slice(r * NDEV, (r + 1) * NDEV)
        here = sub[:CAP] == rank
        ohs[:, cols] = ohb
        vhi[:, cols] = jnp.where(here, code_hi[r:r + 1], 0.0).astype(BF16)
        vlo[:, cols] = jnp.where(here, code_lo[r:r + 1], 0.0).astype(BF16)
        vbag[:, cols] = jnp.where(sub % CAP == rank, bag[r:r + 1], 0.0).astype(BF16)
    all_oh = ohs[...]
    box = dot(all_oh, vhi[...], NT_DIMS) * 256.0 + dot(all_oh, vlo[...], NT_DIMS)
    outbox[...] = box.astype(I32).reshape(8, 16, 1, CAP)

    pl.semaphore_wait(barrier, 22)

    def line_copy(n):
        return pltpu.make_async_remote_copy(
            src_ref=outbox.at[n], dst_ref=passing.at[:, n], send_sem=ids_send.at[0], recv_sem=ids_recv.at[0],
            device_id=line[n], device_id_type=MESH)

    def plane_copy(n):
        return pltpu.make_async_remote_copy(
            src_ref=passing.at[n], dst_ref=inbox.at[n], send_sem=ids_send.at[1], recv_sem=ids_recv.at[1],
            device_id=plane[n], device_id_type=MESH)

    for n in range(1, 8):
        line_copy(n).start()
    passing[:, 0] = outbox[0]

    first = pltpu.make_async_remote_copy(
        src_ref=outbox.at[pl.ds(1, 7)], dst_ref=outbox.at[pl.ds(1, 7)], send_sem=ids_send.at[0],
        recv_sem=ids_recv.at[0], device_id=line[1], device_id_type=MESH)
    second = pltpu.make_async_remote_copy(
        src_ref=passing.at[pl.ds(1, 15)], dst_ref=inbox.at[pl.ds(1, 15)], send_sem=ids_send.at[1],
        recv_sem=ids_recv.at[1], device_id=plane[1], device_id_type=MESH)
    first.wait_recv()
    for n in range(1, 16):
        plane_copy(n).start()
    inbox[0] = passing[0]

    def device(kind, da, db, dy, core, sign):
        dx, dz = da + kind * (db - da), db + kind * (da - db)
        return (lax.rem(x + 4 + sign * dx, 4) * 4 + lax.rem(z + 4 + sign * dz, 4), lax.rem(y + 4 + sign * dy, 4) * 2 + core)

    def line_at(t, n):
        return (0, n, t) if n < 3 else (t, 3, 0)

    def line_order(slot):
        dy, dc, dx, dz = slot // 32, slot // 16 % 2, slot // 4 % 4, slot % 4
        da, db = dx + c * (dz - dx), dz + c * (dx - dz)
        on_y = db == 3
        t, member = jnp.where(on_y, da, dy), jnp.where(on_y, dy, da)
        return (t * 4 + db) * 2 + member // 2, member % 2 * 2 + (c + dc) % 2

    bags = dot(all_oh, vbag[...], NT_DIMS)
    bags = jnp.where(lan // CAP == line_order(sub)[1], bags, 0.0).astype(BF16)
    pick = (line_order(lan[:32])[0] == sub[:32]).astype(F32).astype(BF16)
    mybags[...] = dot(pick, bags).astype(I32).reshape(32, 1, NDEV)
    for cp in loads[2:]:
        cp.wait()
    dense = dense_ref[...]
    hidden = lax.dot_general(dense, wd[...], NN_DIMS, precision=lax.Precision.HIGHEST,
                             preferred_element_type=F32) + bias[...]
    for cp in tab_loads:
        cp.wait()

    second.wait_recv()

    def bags_copy(t, n):
        return pltpu.make_async_remote_copy(
            src_ref=mybags.at[pl.ds((t * 4 + n) * 2, 2)], dst_ref=linebags.at[pl.ds((t * 4 + n) * 2, 2)],
            send_sem=bag_send, recv_sem=bag_recv, device_id=device(c, *line_at(t, n), c, 1), device_id_type=MESH)

    for t in range(4):
        for n in range(4):
            if t or n:
                bags_copy(t, n).start()
    linebags[0:2] = mybags[0:2]
    checked[...] = jnp.clip(inbox[...].reshape(NDEV, 1, CAP), 0, tab.shape[0] - 1)
    to_smem = pltpu.make_async_copy(checked, ids, smem_sem)
    to_smem.start()
    to_smem.wait()

    def block(dst, at, e):
        for j in range(CAP):
            dst[(*at, slice(j, j + 1))] = tab[pl.ds(ids[e, 0, j], 1), :]

    def entry(kind, other, da, db, dy):
        return (da * (4 - 3 * kind) + db * (1 + 3 * kind)) * 8 + dy * 2 + other

    def rows_copy(src, dst, t, peer):
        return pltpu.make_async_remote_copy(
            src_ref=src, dst_ref=dst, send_sem=row_send, recv_sem=row_recv.at[t], device_id=peer, device_id_type=MESH)

    @pl.loop(0, 4)
    def _(t):
        for other in range(2):
            kind = c + other * (1 - 2 * c)
            base = (other * 4 + t) * 4

            def gather(m, dst, at):
                for n in range(4):
                    da, db, dy = (m, n, t) if n < 3 else (t, 3, m)
                    block(dst, at(m, n), entry(kind, other, da, db, dy))

            def send(m):
                if m == 0:
                    rows_copy(stage.at[base], agg.at[t, :, 0, c], t, (my_row, y * 2 + kind)).start()
                    return
                rows_copy(stage.at[base + m, pl.ds(0, 3)], agg.at[t, pl.ds(0, 3), m, c], t,
                          device(kind, m, 0, 0, kind, -1)).start()
                rows_copy(stage.at[base + m, 3], agg.at[t, 3, m, c], t, device(kind, 0, 0, m, kind, -1)).start()

            if other == 0:
                gather(0, agg, lambda m, n: (t, n, m, c))

            @pl.loop(1 - other, 4)
            def _(m):
                gather(m, stage, lambda m, n: (base + m, n))
            for m in range(1 - other, 4):
                send(m)

    def count(blocks, sem):
        return pltpu.make_async_remote_copy(
            src_ref=stage.at[pl.ds(0, blocks)], dst_ref=stage.at[pl.ds(0, blocks)], send_sem=sem, recv_sem=sem,
            device_id=line[1], device_id_type=MESH)

    all_bags = pltpu.make_async_remote_copy(
        src_ref=mybags.at[pl.ds(2, 30)], dst_ref=linebags.at[pl.ds(2, 30)], send_sem=bag_send, recv_sem=bag_recv,
        device_id=line[1], device_id_type=MESH)
    all_bags.wait_recv()
    want = lax.broadcasted_iota(I32, (BAGS, NDEV), 0) + 1

    def sum_copy(t, n):
        return pltpu.make_async_remote_copy(
            src_ref=sums.at[t * 4 + n], dst_ref=parts.at[t * 4 + n], send_sem=sum_send, recv_sem=sum_recv.at[t],
            device_id=device(c, *line_at(t, n), c, -1), device_id_type=MESH)

    def sums_of(t):
        begin = 1 if t == 0 else t * 4
        span = pl.ds(begin, t * 4 + 4 - begin)
        return pltpu.make_async_remote_copy(
            src_ref=sums.at[span], dst_ref=parts.at[span], send_sem=sum_send, recv_sem=sum_recv.at[t],
            device_id=line[1], device_id_type=MESH)

    for t in range(4):
        count(7, row_recv.at[t]).wait_recv()
        for n in range(4):
            at = (t * 4 + n) * 2
            w = jnp.concatenate([(want == linebags[at + h]).astype(F32) for h in range(2)], axis=1).astype(BF16)
            hi, lo = split2(agg[t, n].reshape(8 * CAP, E))
            part = dot(w, hi) + dot(w, lo)
            if t or n:
                sums[t * 4 + n] = part
                sum_copy(t, n).start()
            else:
                parts[0] = part

    total = jnp.zeros((BAGS, E), F32)
    for t in range(4):
        sums_of(t).wait_recv()
        for n in range(4):
            total = total + parts[t * 4 + n]

    feats = [dense] + [total[t * 16:(t + 1) * 16] for t in range(NT)]
    for t in range(NT):
        pooled_out[:, t, :] = feats[t + 1]
    k = 0
    for a in range(NT + 1):
        for b in range(a + 1, NT + 1):
            d = jnp.sum(feats[a] * feats[b], axis=-1, keepdims=True)
            hidden = hidden + d * wp[k:k + 1, :]
            k += 1
    hidden_out[...] = jnp.maximum(hidden, 0.0)

    first.wait_send()
    second.wait_send()
    all_bags.wait_send()
    count(28, row_send).wait_send()
    pltpu.make_async_remote_copy(
        src_ref=sums.at[pl.ds(1, 15)], dst_ref=parts.at[pl.ds(1, 15)], send_sem=sum_send, recv_sem=sum_recv.at[0],
        device_id=line[1], device_id_type=MESH).wait_send()


def put_out(pooled, hidden, pooled_out, hidden_out, sems):
    copies = [pltpu.make_async_copy(pooled, pooled_out, sems.at[0]), pltpu.make_async_copy(hidden, hidden_out, sems.at[1])]
    for cp in copies:
        cp.start()
    for cp in copies:
        cp.wait()


def shards(bag_index, bag_length, emb_tables, dense_feats, w_dense, w_pair, top_bias):
    rows = NT * emb_tables.shape[1]
    hidden = w_dense.shape[1]
    slots = 16 * NDEV
    vmem, hbm = pl.BlockSpec(memory_space=pltpu.VMEM), pl.BlockSpec(memory_space=pltpu.HBM)
    outs = (jax.ShapeDtypeStruct((16, NT, E), F32), jax.ShapeDtypeStruct((16, hidden), F32))
    found = pl.pallas_call(
        kernel,
        out_shape=outs,
        in_specs=[hbm] * 7,
        out_specs=(vmem, vmem),
        scratch_shapes=[
            pltpu.VMEM((16, NDEV), I32),
            pltpu.VMEM((NT, 16), I32),
            pltpu.VMEM((rows, E), F32),
            pltpu.VMEM((16, E), F32),
            pltpu.VMEM(w_dense.shape, F32),
            pltpu.VMEM(w_pair.shape, F32),
            pltpu.VMEM((1, hidden), F32),
            pltpu.VMEM((NDEV, slots), BF16),
            pltpu.VMEM((CAP, slots), BF16),
            pltpu.VMEM((CAP, slots), BF16),
            pltpu.VMEM((NDEV, slots), BF16),
            pltpu.VMEM((8, 16, 1, CAP), I32),
            pltpu.VMEM((16, 8, 1, CAP), I32),
            pltpu.VMEM((16, 8, 1, CAP), I32),
            pltpu.VMEM((NDEV, 1, CAP), I32),
            pltpu.SMEM((NDEV, 1, CAP), I32),
            pltpu.VMEM((32, 1, NDEV), I32),
            pltpu.VMEM((32, 1, NDEV), I32),
            pltpu.VMEM((32, 4, CAP, E), F32),
            pltpu.VMEM((4, 4, 4, 2, CAP, E), F32),
            pltpu.VMEM((16, BAGS, E), F32),
            pltpu.VMEM((16, BAGS, E), F32),
            pltpu.SemaphoreType.DMA((6,)),
            pltpu.SemaphoreType.DMA((TAB_PARTS,)),
            pltpu.SemaphoreType.DMA((2,)),
            pltpu.SemaphoreType.DMA((2,)),
            pltpu.SemaphoreType.DMA,
            pltpu.SemaphoreType.DMA,
            pltpu.SemaphoreType.DMA,
            pltpu.SemaphoreType.DMA,
            pltpu.SemaphoreType.DMA((4,)),
            pltpu.SemaphoreType.DMA,
            pltpu.SemaphoreType.DMA((4,)),
        ],
        compiler_params=pltpu.CompilerParams(
            collective_id=0, has_side_effects=True, vmem_limit_bytes=60 * 1024 * 1024),
    )(bag_index, bag_length.T, emb_tables.reshape(rows, E), dense_feats, w_dense, w_pair, top_bias.reshape(1, hidden))
    return pl.pallas_call(
        put_out,
        out_shape=outs,
        in_specs=[vmem, vmem],
        out_specs=(hbm, hbm),
        compiler_params=pltpu.CompilerParams(vmem_limit_bytes=60 * 1024 * 1024),
        scratch_shapes=[pltpu.SemaphoreType.DMA((2,))],
    )(*found)


def solution(mesh):
    samples = P(("rows", "cols"), None)
    in_specs = (samples, samples, P(None, ("rows", "cols"), None), samples, P(), P(), P())
    out_specs = (P(("rows", "cols"), None, None), samples)
    return jax.shard_map(shards, mesh=mesh, in_specs=in_specs, out_specs=out_specs, check_vma=False)
```

time: 54.6 us -> 39.8 us (0.73)
  the two profiles are of different devices: /device:TPU:1 before, /device:TPU:0 now
where the time goes in v2:
time: 39.8 us; the launch traced here: 39.6 us
  Pallas kernels  39 us (98%)
  between operations  0.64 us (2%)
    pallas_call x1, Pallas kernels, shards(): pl.pallas_call(kernel, out_shape=outs, in_specs=[hbm] * 7, out_specs=(vme...  37.5 us
    pallas_call x1, Pallas kernels, shards(): pl.pallas_call(put_out, out_shape=outs, in_specs=[vmem, vmem], out_specs=...  1.52 us

profile of v2, /device:TPU:0, one launch (start us, length us, event | category | flops | bytes accessed | tf_op | source)
XLA Modules:
  0.0 39.6 jit_solution(1231589858511720466)
XLA Ops:
  0.6 37.5 %shard_map.86 = (f32[16,4,128]{2,1,0:T(4,128)}, f32[16,1024]{1,0:T(8,128)}) custom-call(s32[16,128]{1,0:T(8,128)} %idx_hbm.1, s32[4,16]{1,0:T(4,128)} %bitcast.5, f32[32768,128]{1,0:T(8,128)} %bitcast.3, f32[16,128]{1,0:T(8,128)} %dense_hbm.1, f32[128,1024]{1,0:T(8,128)} %wd_hbm.1, f32[10,1024]{1,0:T(8,128)} %wp_hbm.1, f32[1,1024]{1,0:T(1,128)} %bitcast.4), custom_call_target="tpu_custom_call" | custom-call | tf_op jit(solution)/shard_map/pallas_call | solution.py:287
  38.1 1.5 %shard_map.87 = (f32[16,4,128]{2,1,0:T(4,128)}, f32[16,1024]{1,0:T(8,128)}) custom-call(f32[16,4,128]{2,1,0:T(4,128)} %get-tuple-element.4.pooled, f32[16,1024]{1,0:T(8,128)} %get-tuple-element.5.hidden), custom_call_target="tpu_custom_call" | custom-call | tf_op jit(solution)/shard_map/pallas_call | solution.py:330

commit v3 on v2

--- a/solution.py
+++ b/solution.py
@@ -40,7 +40,7 @@
 
 
 def kernel(idx_hbm, len_hbm, tab_hbm, dense_hbm, wd_hbm, wp_hbm, bias_hbm, pooled_out, hidden_out,
-           idx_ref, len_ref, tab, dense_ref, wd, wp, bias, ohs, vhi, vlo, vbag, outbox, passing, inbox, checked, ids, mybags, linebags, stage, agg, sums, parts,
+           idx_ref, len_ref, tab, dense_ref, wd, wp, bias, ohs, vhi, vlo, vbag, outbox, passing, ids, mybags, linebags, stage, agg, sums, parts,
            load_sem, tab_sem, ids_send, ids_recv, smem_sem, bag_send, bag_recv, row_send, row_recv, sum_send, sum_recv):
     me = position()
     loads = [pltpu.make_async_copy(s, d, load_sem.at[n]) for n, (s, d) in
@@ -97,7 +97,7 @@
         vbag[:, cols] = jnp.where(sub % CAP == rank, bag[r:r + 1], 0.0).astype(BF16)
     all_oh = ohs[...]
     box = dot(all_oh, vhi[...], NT_DIMS) * 256.0 + dot(all_oh, vlo[...], NT_DIMS)
-    outbox[...] = box.astype(I32).reshape(8, 16, 1, CAP)
+    outbox[...] = jnp.clip(box.astype(I32), 0, tab.shape[0] - 1).reshape(8, 16, 1, CAP)
 
     pl.semaphore_wait(barrier, 22)
 
@@ -108,7 +108,7 @@
 
     def plane_copy(n):
         return pltpu.make_async_remote_copy(
-            src_ref=passing.at[n], dst_ref=inbox.at[n], send_sem=ids_send.at[1], recv_sem=ids_recv.at[1],
+            src_ref=passing.at[n], dst_ref=ids.at[pl.ds(n * 8, 8)], send_sem=ids_send.at[1], recv_sem=ids_recv.at[1],
             device_id=plane[n], device_id_type=MESH)
 
     for n in range(1, 8):
@@ -119,12 +119,13 @@
         src_ref=outbox.at[pl.ds(1, 7)], dst_ref=outbox.at[pl.ds(1, 7)], send_sem=ids_send.at[0],
         recv_sem=ids_recv.at[0], device_id=line[1], device_id_type=MESH)
     second = pltpu.make_async_remote_copy(
-        src_ref=passing.at[pl.ds(1, 15)], dst_ref=inbox.at[pl.ds(1, 15)], send_sem=ids_send.at[1],
+        src_ref=passing.at[pl.ds(1, 15)], dst_ref=passing.at[pl.ds(1, 15)], send_sem=ids_send.at[1],
         recv_sem=ids_recv.at[1], device_id=plane[1], device_id_type=MESH)
     first.wait_recv()
     for n in range(1, 16):
         plane_copy(n).start()
-    inbox[0] = passing[0]
+    own = pltpu.make_async_copy(passing.at[0], ids.at[pl.ds(0, 8)], smem_sem)
+    own.start()
 
     def device(kind, da, db, dy, core, sign):
         dx, dz = da + kind * (db - da), db + kind * (da - db)
@@ -164,11 +165,7 @@
             if t or n:
                 bags_copy(t, n).start()
     linebags[0:2] = mybags[0:2]
-    checked[...] = jnp.clip(inbox[...].reshape(NDEV, 1, CAP), 0, tab.shape[0] - 1)
-    to_smem = pltpu.make_async_copy(checked, ids, smem_sem)
-    to_smem.start()
-    to_smem.wait()
-
+    own.wait()
     def block(dst, at, e):
         for j in range(CAP):
             dst[(*at, slice(j, j + 1))] = tab[pl.ds(ids[e, 0, j], 1), :]
@@ -303,8 +300,6 @@
             pltpu.VMEM((NDEV, slots), BF16),
             pltpu.VMEM((8, 16, 1, CAP), I32),
             pltpu.VMEM((16, 8, 1, CAP), I32),
-            pltpu.VMEM((16, 8, 1, CAP), I32),
-            pltpu.VMEM((NDEV, 1, CAP), I32),
             pltpu.SMEM((NDEV, 1, CAP), I32),
             pltpu.VMEM((32, 1, NDEV), I32),
             pltpu.VMEM((32, 1, NDEV), I32),
@@ -325,16 +320,17 @@
             pltpu.SemaphoreType.DMA((4,)),
         ],
         compiler_params=pltpu.CompilerParams(
-            collective_id=0, has_side_effects=True, vmem_limit_bytes=60 * 1024 * 1024),
-    )(bag_index, bag_length.T, emb_tables.reshape(rows, E), dense_feats, w_dense, w_pair, top_bias.reshape(1, hidden))
+            collective_id=0, has_side_effects=True, vmem_limit_bytes=40 * 1024 * 1024),
+    )(*[pltpu.with_memory_space_constraint(a, pltpu.HBM) for a in (
+        bag_index, bag_length.T, emb_tables.reshape(rows, E), dense_feats, w_dense, w_pair,
+        top_bias.reshape(1, hidden))])
     return pl.pallas_call(
         put_out,
         out_shape=outs,
         in_specs=[vmem, vmem],
         out_specs=(hbm, hbm),
-        compiler_params=pltpu.CompilerParams(vmem_limit_bytes=60 * 1024 * 1024),
         scratch_shapes=[pltpu.SemaphoreType.DMA((2,))],
-    )(*found)
+    )(*[pltpu.with_memory_space_constraint(a, pltpu.VMEM) for a in found])
 
 
 def solution(mesh):

time: 39.8 us -> 36.6 us (0.920)
  Pallas kernels: 39 us -> 35.9 us
    pallas_call x1, Pallas kernels: 37.5 us -> 35.2 us  [shards(): pl.pallas_call(kernel, out_shape=outs, in_specs=[hbm] * 7, out_specs=(vme...]
    pallas_call x1, Pallas kernels: 1.52 us -> 0.66 us  [shards(): pl.pallas_call(put_out, out_shape=outs, in_specs=[vmem, vmem], out_specs=...]
where the time goes in v3:
time: 36.6 us; the launch traced here: 36.5 us
  Pallas kernels  35.9 us (98%)
  between operations  0.64 us (2%)
    pallas_call x1, Pallas kernels, shards(): pl.pallas_call(kernel, out_shape=outs, in_specs=[hbm] * 7, out_specs=(vme...  35.2 us

profile of v3, /device:TPU:0, one launch (start us, length us, event | category | flops | bytes accessed | tf_op | source)
XLA Modules:
  0.0 36.5 jit_solution(9680015898769397020)
XLA Ops:
  0.6 35.2 %shard_map.86 = (f32[16,4,128]{2,1,0:T(4,128)S(1)}, f32[16,1024]{1,0:T(8,128)S(1)}) custom-call(s32[16,128]{1,0:T(8,128)} %idx_hbm.1, s32[4,16]{1,0:T(4,128)} %bitcast.5, f32[32768,128]{1,0:T(8,128)} %bitcast.3, f32[16,128]{1,0:T(8,128)} %dense_hbm.1, f32[128,1024]{1,0:T(8,128)} %wd_hbm.1, f32[10,1024]{1,0:T(8,128)} %wp_hbm.1, f32[1,1024]{1,0:T(1,128)} %bitcast.4), custom_call_target="tpu_custom_call" | custom-call | tf_op jit(solution)/shard_map/pallas_call | solution.py:284
  35.9 0.7 %shard_map.87 = (f32[16,4,128]{2,1,0:T(4,128)}, f32[16,1024]{1,0:T(8,128)}) custom-call(f32[16,4,128]{2,1,0:T(4,128)S(1)} %get-tuple-element.4.pooled, f32[16,1024]{1,0:T(8,128)S(1)} %get-tuple-element.5.hidden), custom_call_target="tpu_custom_call" | custom-call | tf_op jit(solution)/shard_map/pallas_call | solution.py:327

commit v4 on v3

--- a/solution.py
+++ b/solution.py
@@ -40,7 +40,7 @@
 
 
 def kernel(idx_hbm, len_hbm, tab_hbm, dense_hbm, wd_hbm, wp_hbm, bias_hbm, pooled_out, hidden_out,
-           idx_ref, len_ref, tab, dense_ref, wd, wp, bias, ohs, vhi, vlo, vbag, outbox, passing, ids, mybags, linebags, stage, agg, sums, parts,
+           idx_ref, len_ref, tab, dense_ref, wd, wp, bias, ohs, vcode, vbag, outbox, passing, ids, mybags, linebags, stage, agg, sums, parts,
            load_sem, tab_sem, ids_send, ids_recv, smem_sem, bag_send, bag_recv, row_send, row_recv, sum_send, sum_recv):
     me = position()
     loads = [pltpu.make_async_copy(s, d, load_sem.at[n]) for n, (s, d) in
@@ -83,6 +83,7 @@
     before = jnp.concatenate([(sub < lan).astype(F32), jnp.ones((NDEV, NDEV), F32)], axis=1).astype(BF16)
     code_hi, code_lo, bag = (code // 256).astype(F32), (code % 256).astype(F32), bag.astype(F32)
     carry = jnp.zeros((NDEV, NDEV), F32)
+    ranks = []
     for r in range(16):
         oh = (sub == rel[r:r + 1, :]).astype(F32)
         ohb = oh.astype(BF16)
@@ -92,11 +93,12 @@
         cols = slice(r * NDEV, (r + 1) * NDEV)
         here = sub[:CAP] == rank
         ohs[:, cols] = ohb
-        vhi[:, cols] = jnp.where(here, code_hi[r:r + 1], 0.0).astype(BF16)
-        vlo[:, cols] = jnp.where(here, code_lo[r:r + 1], 0.0).astype(BF16)
-        vbag[:, cols] = jnp.where(sub % CAP == rank, bag[r:r + 1], 0.0).astype(BF16)
+        vcode[:CAP, cols] = jnp.where(here, code_hi[r:r + 1], 0.0).astype(BF16)
+        vcode[CAP:, cols] = jnp.where(here, code_lo[r:r + 1], 0.0).astype(BF16)
+        ranks.append(rank)
     all_oh = ohs[...]
-    box = dot(all_oh, vhi[...], NT_DIMS) * 256.0 + dot(all_oh, vlo[...], NT_DIMS)
+    box = dot(all_oh, vcode[...], NT_DIMS)
+    box = box[:, :CAP] * 256.0 + box[:, CAP:]
     outbox[...] = jnp.clip(box.astype(I32), 0, tab.shape[0] - 1).reshape(8, 16, 1, CAP)
 
     pl.semaphore_wait(barrier, 22)
@@ -141,6 +143,8 @@
         t, member = jnp.where(on_y, da, dy), jnp.where(on_y, dy, da)
         return (t * 4 + db) * 2 + member // 2, member % 2 * 2 + (c + dc) % 2
 
+    for r in range(16):
+        vbag[:, r * NDEV:(r + 1) * NDEV] = jnp.where(sub % CAP == ranks[r], bag[r:r + 1], 0.0).astype(BF16)
     bags = dot(all_oh, vbag[...], NT_DIMS)
     bags = jnp.where(lan // CAP == line_order(sub)[1], bags, 0.0).astype(BF16)
     pick = (line_order(lan[:32])[0] == sub[:32]).astype(F32).astype(BF16)
@@ -177,33 +181,25 @@
         return pltpu.make_async_remote_copy(
             src_ref=src, dst_ref=dst, send_sem=row_send, recv_sem=row_recv.at[t], device_id=peer, device_id_type=MESH)
 
-    @pl.loop(0, 4)
-    def _(t):
-        for other in range(2):
+    def push(t):
+        def gather(kind, other, m, dst, at):
+            for n in range(4):
+                da, db, dy = (m, n, t) if n < 3 else (t, 3, m)
+                block(dst, at(n), entry(kind, other, da, db, dy))
+
+        @pl.loop(0, 6)
+        def _(i):
+            other, m = lax.rem(i, 2), lax.div(i, 2) + 1
             kind = c + other * (1 - 2 * c)
-            base = (other * 4 + t) * 4
-
-            def gather(m, dst, at):
-                for n in range(4):
-                    da, db, dy = (m, n, t) if n < 3 else (t, 3, m)
-                    block(dst, at(m, n), entry(kind, other, da, db, dy))
-
-            def send(m):
-                if m == 0:
-                    rows_copy(stage.at[base], agg.at[t, :, 0, c], t, (my_row, y * 2 + kind)).start()
-                    return
-                rows_copy(stage.at[base + m, pl.ds(0, 3)], agg.at[t, pl.ds(0, 3), m, c], t,
-                          device(kind, m, 0, 0, kind, -1)).start()
-                rows_copy(stage.at[base + m, 3], agg.at[t, 3, m, c], t, device(kind, 0, 0, m, kind, -1)).start()
-
-            if other == 0:
-                gather(0, agg, lambda m, n: (t, n, m, c))
-
-            @pl.loop(1 - other, 4)
-            def _(m):
-                gather(m, stage, lambda m, n: (base + m, n))
-            for m in range(1 - other, 4):
-                send(m)
+            at = (other * 4 + t) * 4 + m
+            gather(kind, other, m, stage, lambda n: (at, n))
+            rows_copy(stage.at[at, pl.ds(0, 3)], agg.at[t, pl.ds(0, 3), m, c], t,
+                      device(kind, m, 0, 0, kind, -1)).start()
+            rows_copy(stage.at[at, 3], agg.at[t, 3, m, c], t, device(kind, 0, 0, m, kind, -1)).start()
+
+        gather(1 - c, 1, 0, stage, lambda n: ((4 + t) * 4, n))
+        rows_copy(stage.at[(4 + t) * 4], agg.at[t, :, 0, c], t, (my_row, y * 2 + 1 - c)).start()
+        gather(c, 0, 0, agg, lambda n: (t, n, 0, c))
 
     def count(blocks, sem):
         return pltpu.make_async_remote_copy(
@@ -213,7 +209,6 @@
     all_bags = pltpu.make_async_remote_copy(
         src_ref=mybags.at[pl.ds(2, 30)], dst_ref=linebags.at[pl.ds(2, 30)], send_sem=bag_send, recv_sem=bag_recv,
         device_id=line[1], device_id_type=MESH)
-    all_bags.wait_recv()
     want = lax.broadcasted_iota(I32, (BAGS, NDEV), 0) + 1
 
     def sum_copy(t, n):
@@ -228,9 +223,9 @@
             src_ref=sums.at[span], dst_ref=parts.at[span], send_sem=sum_send, recv_sem=sum_recv.at[t],
             device_id=line[1], device_id_type=MESH)
 
-    for t in range(4):
+    def pool(t):
         count(7, row_recv.at[t]).wait_recv()
-        for n in range(4):
+        for n in (2, 1, 3, 0):
             at = (t * 4 + n) * 2
             w = jnp.concatenate([(want == linebags[at + h]).astype(F32) for h in range(2)], axis=1).astype(BF16)
             hi, lo = split2(agg[t, n].reshape(8 * CAP, E))
@@ -241,8 +236,15 @@
             else:
                 parts[0] = part
 
+    order = (2, 1, 3, 0)
+    for t in order:
+        push(t)
+    all_bags.wait_recv()
+    for t in order:
+        pool(t)
+
     total = jnp.zeros((BAGS, E), F32)
-    for t in range(4):
+    for t in order:
         sums_of(t).wait_recv()
         for n in range(4):
             total = total + parts[t * 4 + n]
@@ -295,8 +297,7 @@
             pltpu.VMEM(w_pair.shape, F32),
             pltpu.VMEM((1, hidden), F32),
             pltpu.VMEM((NDEV, slots), BF16),
-            pltpu.VMEM((CAP, slots), BF16),
-            pltpu.VMEM((CAP, slots), BF16),
+            pltpu.VMEM((2 * CAP, slots), BF16),
             pltpu.VMEM((NDEV, slots), BF16),
             pltpu.VMEM((8, 16, 1, CAP), I32),
             pltpu.VMEM((16, 8, 1, CAP), I32),

time: 36.6 us -> 34.8 us (0.951)
  Pallas kernels: 35.9 us -> 34 us
    pallas_call x1, Pallas kernels: 35.2 us -> 33.4 us  [shards(): pl.pallas_call(kernel, out_shape=outs, in_specs=[hbm] * 7, out_specs=(vme...]
where the time goes in v4:
time: 34.8 us; the launch traced here: 34.7 us
  Pallas kernels  34 us (98%)
  between operations  0.64 us (2%)
    pallas_call x1, Pallas kernels, shards(): pl.pallas_call(kernel, out_shape=outs, in_specs=[hbm] * 7, out_specs=(vme...  33.4 us

profile of v4, /device:TPU:0, one launch (start us, length us, event | category | flops | bytes accessed | tf_op | source)
XLA Modules:
  0.0 34.7 jit_solution(3981525444692966769)
XLA Ops:
  0.6 33.4 %shard_map.86 = (f32[16,4,128]{2,1,0:T(4,128)S(1)}, f32[16,1024]{1,0:T(8,128)S(1)}) custom-call(s32[16,128]{1,0:T(8,128)} %idx_hbm.1, s32[4,16]{1,0:T(4,128)} %bitcast.5, f32[32768,128]{1,0:T(8,128)} %bitcast.3, f32[16,128]{1,0:T(8,128)} %dense_hbm.1, f32[128,1024]{1,0:T(8,128)} %wd_hbm.1, f32[10,1024]{1,0:T(8,128)} %wp_hbm.1, f32[1,1024]{1,0:T(1,128)} %bitcast.4), custom_call_target="tpu_custom_call" | custom-call | tf_op jit(solution)/shard_map/pallas_call | solution.py:286
  34.0 0.7 %shard_map.87 = (f32[16,4,128]{2,1,0:T(4,128)}, f32[16,1024]{1,0:T(8,128)}) custom-call(f32[16,4,128]{2,1,0:T(4,128)S(1)} %get-tuple-element.4.pooled, f32[16,1024]{1,0:T(8,128)S(1)} %get-tuple-element.5.hidden), custom_call_target="tpu_custom_call" | custom-call | tf_op jit(solution)/shard_map/pallas_call | solution.py:328

commit v5 on v4

--- a/solution.py
+++ b/solution.py
@@ -14,6 +14,8 @@
 CAP = 32
 BAGS = 64
 TAB_PARTS = 8
+EARLY = 2
+PLANE_PAIRS = ((0, 1), (0, 3), (0, 2), (1, 1), (1, 3), (3, 3), (1, 2), (2, 3), (2, 2), (0, 0))
 MESH = pl.DeviceIdType.MESH
 F32, BF16, I32 = jnp.float32, jnp.bfloat16, jnp.int32
 NT_DIMS = (((1,), (1,)), ((), ()))
@@ -110,7 +112,7 @@
 
     def plane_copy(n):
         return pltpu.make_async_remote_copy(
-            src_ref=passing.at[n], dst_ref=ids.at[pl.ds(n * 8, 8)], send_sem=ids_send.at[1], recv_sem=ids_recv.at[1],
+            src_ref=passing.at[n], dst_ref=ids.at[pl.ds(n * 8, 8)], send_sem=ids_send.at[1], recv_sem=ids_recv.at[n],
             device_id=plane[n], device_id_type=MESH)
 
     for n in range(1, 8):
@@ -120,9 +122,6 @@
     first = pltpu.make_async_remote_copy(
         src_ref=outbox.at[pl.ds(1, 7)], dst_ref=outbox.at[pl.ds(1, 7)], send_sem=ids_send.at[0],
         recv_sem=ids_recv.at[0], device_id=line[1], device_id_type=MESH)
-    second = pltpu.make_async_remote_copy(
-        src_ref=passing.at[pl.ds(1, 15)], dst_ref=passing.at[pl.ds(1, 15)], send_sem=ids_send.at[1],
-        recv_sem=ids_recv.at[1], device_id=plane[1], device_id_type=MESH)
     first.wait_recv()
     for n in range(1, 16):
         plane_copy(n).start()
@@ -157,19 +156,12 @@
     for cp in tab_loads:
         cp.wait()
 
-    second.wait_recv()
 
     def bags_copy(t, n):
         return pltpu.make_async_remote_copy(
             src_ref=mybags.at[pl.ds((t * 4 + n) * 2, 2)], dst_ref=linebags.at[pl.ds((t * 4 + n) * 2, 2)],
             send_sem=bag_send, recv_sem=bag_recv, device_id=device(c, *line_at(t, n), c, 1), device_id_type=MESH)
 
-    for t in range(4):
-        for n in range(4):
-            if t or n:
-                bags_copy(t, n).start()
-    linebags[0:2] = mybags[0:2]
-    own.wait()
     def block(dst, at, e):
         for j in range(CAP):
             dst[(*at, slice(j, j + 1))] = tab[pl.ds(ids[e, 0, j], 1), :]
@@ -200,6 +192,44 @@
         gather(1 - c, 1, 0, stage, lambda n: ((4 + t) * 4, n))
         rows_copy(stage.at[(4 + t) * 4], agg.at[t, :, 0, c], t, (my_row, y * 2 + 1 - c)).start()
         gather(c, 0, 0, agg, lambda n: (t, n, 0, c))
+
+    order = (2, 1, 3, 0)
+
+    def push_early(ts):
+        def one(t, other, m, n, dst, at):
+            da, db, dy = (m, n, t) if n < 3 else (t, 3, m)
+            block(dst, at, entry(c + other * (1 - 2 * c), other, da, db, dy))
+
+        waited = set()
+        for u, v in PLANE_PAIRS:
+            for p in sorted({u * 4 + v, v * 4 + u} - waited):
+                waited.add(p)
+                if p:
+                    plane_copy(p).wait_recv()
+                else:
+                    own.wait()
+            if (u, v) == (0, 2):
+                for q in order:
+                    for n in (2, 1, 3, 0):
+                        if q or n:
+                            bags_copy(q, n).start()
+                linebags[0:2] = mybags[0:2]
+            spots = [(t, m, n) for t in ts for m, n in sorted({(u, v), (v, u)}) if n < 3]
+            if 3 in (u, v):
+                spots += [(t, m, 3) for t in ts if t == u + v - 3 for m in range(4)]
+            for t, m, n in spots:
+                if m:
+                    @pl.loop(0, 2)
+                    def _(other):
+                        kind = c + other * (1 - 2 * c)
+                        at = (other * 4 + t) * 4 + m
+                        one(t, other, m, n, stage, (at, n))
+                        away = (m, 0, 0) if n < 3 else (0, 0, m)
+                        rows_copy(stage.at[at, n], agg.at[t, n, m, c], t, device(kind, *away, kind, -1)).start()
+                else:
+                    one(t, 1, 0, n, stage, ((4 + t) * 4, n))
+                    rows_copy(stage.at[(4 + t) * 4, n], agg.at[t, n, 0, c], t, (my_row, y * 2 + 1 - c)).start()
+                    one(t, 0, 0, n, agg, (t, n, 0, c))
 
     def count(blocks, sem):
         return pltpu.make_async_remote_copy(
@@ -236,8 +266,8 @@
             else:
                 parts[0] = part
 
-    order = (2, 1, 3, 0)
-    for t in order:
+    push_early(order[:EARLY])
+    for t in order[EARLY:]:
         push(t)
     all_bags.wait_recv()
     for t in order:
@@ -261,7 +291,9 @@
     hidden_out[...] = jnp.maximum(hidden, 0.0)
 
     first.wait_send()
-    second.wait_send()
+    pltpu.make_async_remote_copy(
+        src_ref=passing.at[pl.ds(1, 15)], dst_ref=passing.at[pl.ds(1, 15)], send_sem=ids_send.at[1],
+        recv_sem=ids_recv.at[1], device_id=plane[1], device_id_type=MESH).wait_send()
     all_bags.wait_send()
     count(28, row_send).wait_send()
     pltpu.make_async_remote_copy(
@@ -311,7 +343,7 @@
             pltpu.SemaphoreType.DMA((6,)),
             pltpu.SemaphoreType.DMA((TAB_PARTS,)),
             pltpu.SemaphoreType.DMA((2,)),
-            pltpu.SemaphoreType.DMA((2,)),
+            pltpu.SemaphoreType.DMA((16,)),
             pltpu.SemaphoreType.DMA,
             pltpu.SemaphoreType.DMA,
             pltpu.SemaphoreType.DMA,

time: 34.8 us -> 33.6 us (0.966)
  Pallas kernels: 34 us -> 32.8 us
    pallas_call x1, Pallas kernels: 33.4 us -> 32.1 us  [shards(): pl.pallas_call(kernel, out_shape=outs, in_specs=[hbm] * 7, out_specs=(vme...]
where the time goes in v5:
time: 33.6 us; the launch traced here: 33.4 us
  Pallas kernels  32.8 us (98%)
  between operations  0.64 us (2%)
    pallas_call x1, Pallas kernels, shards(): pl.pallas_call(kernel, out_shape=outs, in_specs=[hbm] * 7, out_specs=(vme...  32.1 us

profile of v5, /device:TPU:0, one launch (start us, length us, event | category | flops | bytes accessed | tf_op | source)
XLA Modules:
  0.0 33.4 jit_solution(17738119131830761679)
XLA Ops:
  0.6 32.1 %shard_map.86 = (f32[16,4,128]{2,1,0:T(4,128)S(1)}, f32[16,1024]{1,0:T(8,128)S(1)}) custom-call(s32[16,128]{1,0:T(8,128)} %idx_hbm.1, s32[4,16]{1,0:T(4,128)} %bitcast.5, f32[32768,128]{1,0:T(8,128)} %bitcast.3, f32[16,128]{1,0:T(8,128)} %dense_hbm.1, f32[128,1024]{1,0:T(8,128)} %wd_hbm.1, f32[10,1024]{1,0:T(8,128)} %wp_hbm.1, f32[1,1024]{1,0:T(1,128)} %bitcast.4), custom_call_target="tpu_custom_call" | custom-call | tf_op jit(solution)/shard_map/pallas_call | solution.py:318
  32.8 0.7 %shard_map.87 = (f32[16,4,128]{2,1,0:T(4,128)}, f32[16,1024]{1,0:T(8,128)}) custom-call(f32[16,4,128]{2,1,0:T(4,128)S(1)} %get-tuple-element.4.pooled, f32[16,1024]{1,0:T(8,128)S(1)} %get-tuple-element.5.hidden), custom_call_target="tpu_custom_call" | custom-call | tf_op jit(solution)/shard_map/pallas_call | solution.py:360

commit v6 on v4

--- a/solution.py
+++ b/solution.py
@@ -14,6 +14,10 @@
 CAP = 32
 BAGS = 64
 TAB_PARTS = 8
+NEAR, FAR = (0, 1, 3), 2
+ORDER, EARLY = (2, 1, 3, 0), 2
+FAR_LINES = {2: (2,), 1: (1,), 3: (3, 0), 0: ()}
+PLANE_PAIRS = ((0, 0), (0, 1), (0, 3), (1, 1), (1, 3), (3, 3), (0, 2), (1, 2), (2, 3), (2, 2))
 MESH = pl.DeviceIdType.MESH
 F32, BF16, I32 = jnp.float32, jnp.bfloat16, jnp.int32
 NT_DIMS = (((1,), (1,)), ((), ()))
@@ -40,7 +44,7 @@
 
 
 def kernel(idx_hbm, len_hbm, tab_hbm, dense_hbm, wd_hbm, wp_hbm, bias_hbm, pooled_out, hidden_out,
-           idx_ref, len_ref, tab, dense_ref, wd, wp, bias, ohs, vcode, vbag, outbox, passing, ids, mybags, linebags, stage, agg, sums, parts,
+           idx_ref, len_ref, tab, dense_ref, wd, wp, bias, ohs, vcode, vbag, outbox, passing, ids, mybags, bagpass, linebags, stage, agg, sums, parts,
            load_sem, tab_sem, ids_send, ids_recv, smem_sem, bag_send, bag_recv, row_send, row_recv, sum_send, sum_recv):
     me = position()
     loads = [pltpu.make_async_copy(s, d, load_sem.at[n]) for n, (s, d) in
@@ -58,9 +62,8 @@
     xs, zs, ys, cs = [around(at, n) for at, n in zip(me, (4, 4, 4, 2))]
     line = [(my_row, y * 2 + c) for y in ys for c in cs]
     plane = [(x * 4 + z, my_col) for x in xs for z in zs]
-    for peer in plane[1:] + line[1:]:
+    for peer in plane[:0:-1] + line[:0:-1]:
         pl.semaphore_signal(barrier, inc=1, device_id=peer, device_id_type=MESH)
-
 
     for cp in loads[:2]:
         cp.wait()
@@ -105,43 +108,35 @@
 
     def line_copy(n):
         return pltpu.make_async_remote_copy(
-            src_ref=outbox.at[n], dst_ref=passing.at[:, n], send_sem=ids_send.at[0], recv_sem=ids_recv.at[0],
+            src_ref=outbox.at[n], dst_ref=passing.at[:, n // 2 * 2 + c], send_sem=ids_send.at[0], recv_sem=ids_recv.at[0],
             device_id=line[n], device_id_type=MESH)
 
     def plane_copy(n):
         return pltpu.make_async_remote_copy(
-            src_ref=passing.at[n], dst_ref=ids.at[pl.ds(n * 8, 8)], send_sem=ids_send.at[1], recv_sem=ids_recv.at[1],
+            src_ref=passing.at[n], dst_ref=ids.at[pl.ds(n * 8, 8)], send_sem=ids_send.at[1], recv_sem=ids_recv.at[n],
             device_id=plane[n], device_id_type=MESH)
 
     for n in range(1, 8):
         line_copy(n).start()
-    passing[:, 0] = outbox[0]
+    passing[:, pl.ds(c, 1)] = outbox[0].reshape(16, 1, 1, CAP)
 
     first = pltpu.make_async_remote_copy(
         src_ref=outbox.at[pl.ds(1, 7)], dst_ref=outbox.at[pl.ds(1, 7)], send_sem=ids_send.at[0],
         recv_sem=ids_recv.at[0], device_id=line[1], device_id_type=MESH)
-    second = pltpu.make_async_remote_copy(
-        src_ref=passing.at[pl.ds(1, 15)], dst_ref=passing.at[pl.ds(1, 15)], send_sem=ids_send.at[1],
-        recv_sem=ids_recv.at[1], device_id=plane[1], device_id_type=MESH)
-    first.wait_recv()
-    for n in range(1, 16):
-        plane_copy(n).start()
-    own = pltpu.make_async_copy(passing.at[0], ids.at[pl.ds(0, 8)], smem_sem)
-    own.start()
-
     def device(kind, da, db, dy, core, sign):
         dx, dz = da + kind * (db - da), db + kind * (da - db)
         return (lax.rem(x + 4 + sign * dx, 4) * 4 + lax.rem(z + 4 + sign * dz, 4), lax.rem(y + 4 + sign * dy, 4) * 2 + core)
 
     def line_at(t, n):
-        return (0, n, t) if n < 3 else (t, 3, 0)
+        return (0, NEAR[n], t) if n < 3 else (t, FAR, 0)
 
     def line_order(slot):
         dy, dc, dx, dz = slot // 32, slot // 16 % 2, slot // 4 % 4, slot % 4
         da, db = dx + c * (dz - dx), dz + c * (dx - dz)
-        on_y = db == 3
+        on_y = db == FAR
+        n = jnp.where(db >= FAR, FAR + 3 - db, db)
         t, member = jnp.where(on_y, da, dy), jnp.where(on_y, dy, da)
-        return (t * 4 + db) * 2 + member // 2, member % 2 * 2 + (c + dc) % 2
+        return (t * 4 + n) * 2 + member // 2, member % 2 * 2 + (c + dc) % 2
 
     for r in range(16):
         vbag[:, r * NDEV:(r + 1) * NDEV] = jnp.where(sub % CAP == ranks[r], bag[r:r + 1], 0.0).astype(BF16)
@@ -149,6 +144,36 @@
     bags = jnp.where(lan // CAP == line_order(sub)[1], bags, 0.0).astype(BF16)
     pick = (line_order(lan[:32])[0] == sub[:32]).astype(F32).astype(BF16)
     mybags[...] = dot(pick, bags).astype(I32).reshape(32, 1, NDEV)
+
+    def bags_copy(src, t, n, peer):
+        return pltpu.make_async_remote_copy(
+            src_ref=src, dst_ref=linebags.at[pl.ds((t * 4 + n) * 2, 2)], send_sem=bag_send.at[1],
+            recv_sem=bag_recv.at[1], device_id=peer, device_id_type=MESH)
+
+    def relay_copy(t):
+        return pltpu.make_async_remote_copy(
+            src_ref=mybags.at[pl.ds(t * 8, 6)], dst_ref=bagpass.at[pl.ds((t - 1) * 6, 6)], send_sem=bag_send.at[0],
+            recv_sem=bag_recv.at[0], device_id=(my_row, ys[t] * 2 + c), device_id_type=MESH)
+
+    for t in range(1, 4):
+        relay_copy(t).start()
+    for t, n in ((0, 1), (0, 2), (0, 3), (1, 3), (2, 3), (3, 3)):
+        bags_copy(mybags.at[pl.ds((t * 4 + n) * 2, 2)], t, n, device(c, *line_at(t, n), c, 1)).start()
+    linebags[0:2] = mybags[0:2]
+    first.wait_recv()
+    for n in range(1, 16):
+        plane_copy(n).start()
+    own = pltpu.make_async_copy(passing.at[0], ids.at[pl.ds(0, 8)], smem_sem)
+    own.start()
+    relayed = pltpu.make_async_remote_copy(
+        src_ref=bagpass.at[pl.ds(0, 18)], dst_ref=bagpass.at[pl.ds(0, 18)], send_sem=bag_send.at[0],
+        recv_sem=bag_recv.at[0], device_id=line[1], device_id_type=MESH)
+    relayed.wait_recv()
+    for t in range(1, 4):
+        linebags[t * 8:t * 8 + 2] = bagpass[(t - 1) * 6:(t - 1) * 6 + 2]
+        for n in (1, 2):
+            bags_copy(bagpass.at[pl.ds((t - 1) * 6 + n * 2, 2)], t, n, device(c, 0, NEAR[n], 0, c, 1)).start()
+
     for cp in loads[2:]:
         cp.wait()
     dense = dense_ref[...]
@@ -157,49 +182,71 @@
     for cp in tab_loads:
         cp.wait()
 
-    second.wait_recv()
-
-    def bags_copy(t, n):
-        return pltpu.make_async_remote_copy(
-            src_ref=mybags.at[pl.ds((t * 4 + n) * 2, 2)], dst_ref=linebags.at[pl.ds((t * 4 + n) * 2, 2)],
-            send_sem=bag_send, recv_sem=bag_recv, device_id=device(c, *line_at(t, n), c, 1), device_id_type=MESH)
-
-    for t in range(4):
-        for n in range(4):
-            if t or n:
-                bags_copy(t, n).start()
-    linebags[0:2] = mybags[0:2]
-    own.wait()
+
     def block(dst, at, e):
         for j in range(CAP):
             dst[(*at, slice(j, j + 1))] = tab[pl.ds(ids[e, 0, j], 1), :]
 
-    def entry(kind, other, da, db, dy):
-        return (da * (4 - 3 * kind) + db * (1 + 3 * kind)) * 8 + dy * 2 + other
-
     def rows_copy(src, dst, t, peer):
         return pltpu.make_async_remote_copy(
             src_ref=src, dst_ref=dst, send_sem=row_send, recv_sem=row_recv.at[t], device_id=peer, device_id_type=MESH)
 
+    def spot(t, n, m):
+        return (m, NEAR[n], t) if n < 3 else (t, FAR, m)
+
+    def stage_at(kind, t, n, m):
+        return ((kind * 4 + m) * 4 + n) * 4 + t
+
+    def take(kind, t, n, m):
+        da, db, dy = spot(t, n, m)
+        block(stage, (stage_at(kind, t, n, m),), ((db * 4 + da) if kind else (da * 4 + db)) * 8 + dy * 2 + kind)
+
+    def here(chunk, kind, t, n):
+        at = stage_at(kind, t, n, 0)
+
+        @pl.when(c == kind)
+        def _():
+            agg[t, n, 0, kind] = stage[at]
+
+        @pl.when(c != kind)
+        def _():
+            rows_copy(stage.at[at], agg.at[t, n, 0, 1 - kind], chunk, (my_row, y * 2 + kind)).start()
+
     def push(t):
-        def gather(kind, other, m, dst, at):
-            for n in range(4):
-                da, db, dy = (m, n, t) if n < 3 else (t, 3, m)
-                block(dst, at(n), entry(kind, other, da, db, dy))
-
-        @pl.loop(0, 6)
-        def _(i):
-            other, m = lax.rem(i, 2), lax.div(i, 2) + 1
-            kind = c + other * (1 - 2 * c)
-            at = (other * 4 + t) * 4 + m
-            gather(kind, other, m, stage, lambda n: (at, n))
-            rows_copy(stage.at[at, pl.ds(0, 3)], agg.at[t, pl.ds(0, 3), m, c], t,
-                      device(kind, m, 0, 0, kind, -1)).start()
-            rows_copy(stage.at[at, 3], agg.at[t, 3, m, c], t, device(kind, 0, 0, m, kind, -1)).start()
-
-        gather(1 - c, 1, 0, stage, lambda n: ((4 + t) * 4, n))
-        rows_copy(stage.at[(4 + t) * 4], agg.at[t, :, 0, c], t, (my_row, y * 2 + 1 - c)).start()
-        gather(c, 0, 0, agg, lambda n: (t, n, 0, c))
+        lines = [(t, n) for n in range(3)] + [(a, 3) for a in FAR_LINES[t]]
+        for m in (1, 2, 3, 0):
+            for kind in range(2):
+                for a, n in lines:
+                    take(kind, a, n, m)
+                    if m:
+                        away = (m, 0, 0) if n < 3 else (0, 0, m)
+                        rows_copy(stage.at[stage_at(kind, a, n, m)], agg.at[a, n, m, c], t,
+                                  device(kind, *away, kind, -1)).start()
+                    else:
+                        here(t, kind, a, n)
+
+    def push_early(ts):
+        waited = set()
+        for u, v in PLANE_PAIRS:
+            for p in sorted({u * 4 + v, v * 4 + u} - waited):
+                waited.add(p)
+                if p:
+                    plane_copy(p).wait_recv()
+                else:
+                    own.wait()
+            for t in ts:
+                spots = [(t, NEAR.index(b), m) for m, b in sorted({(u, v), (v, u)}) if b in NEAR]
+                if FAR in (u, v) and u + v - FAR in FAR_LINES[t]:
+                    spots += [(u + v - FAR, 3, m) for m in range(4)]
+                for a, n, m in spots:
+                    for kind in range(2):
+                        take(kind, a, n, m)
+                        if m:
+                            away = (m, 0, 0) if n < 3 else (0, 0, m)
+                            rows_copy(stage.at[stage_at(kind, a, n, m)], agg.at[a, n, m, c], t,
+                                      device(kind, *away, kind, -1)).start()
+                        else:
+                            here(t, kind, a, n)
 
     def count(blocks, sem):
         return pltpu.make_async_remote_copy(
@@ -207,46 +254,48 @@
             device_id=line[1], device_id_type=MESH)
 
     all_bags = pltpu.make_async_remote_copy(
-        src_ref=mybags.at[pl.ds(2, 30)], dst_ref=linebags.at[pl.ds(2, 30)], send_sem=bag_send, recv_sem=bag_recv,
+        src_ref=mybags.at[pl.ds(0, 24)], dst_ref=linebags.at[pl.ds(0, 24)], send_sem=bag_send.at[1], recv_sem=bag_recv.at[1],
         device_id=line[1], device_id_type=MESH)
     want = lax.broadcasted_iota(I32, (BAGS, NDEV), 0) + 1
 
-    def sum_copy(t, n):
-        return pltpu.make_async_remote_copy(
-            src_ref=sums.at[t * 4 + n], dst_ref=parts.at[t * 4 + n], send_sem=sum_send, recv_sem=sum_recv.at[t],
+    def sum_copy(chunk, t, n):
+        return pltpu.make_async_remote_copy(
+            src_ref=sums.at[t * 4 + n], dst_ref=parts.at[t * 4 + n], send_sem=sum_send, recv_sem=sum_recv.at[chunk],
             device_id=device(c, *line_at(t, n), c, -1), device_id_type=MESH)
 
-    def sums_of(t):
-        begin = 1 if t == 0 else t * 4
-        span = pl.ds(begin, t * 4 + 4 - begin)
-        return pltpu.make_async_remote_copy(
-            src_ref=sums.at[span], dst_ref=parts.at[span], send_sem=sum_send, recv_sem=sum_recv.at[t],
-            device_id=line[1], device_id_type=MESH)
-
-    def pool(t):
-        count(7, row_recv.at[t]).wait_recv()
-        for n in (2, 1, 3, 0):
+    def sums_of(blocks, t):
+        return pltpu.make_async_remote_copy(
+            src_ref=sums.at[pl.ds(0, blocks)], dst_ref=parts.at[pl.ds(0, blocks)], send_sem=sum_send,
+            recv_sem=sum_recv.at[t], device_id=line[1], device_id_type=MESH)
+
+    def chunk_lines(t):
+        return [(a, 3) for a in FAR_LINES[t]] + [(t, n) for n in (2, 1, 0)]
+
+    def pool(chunk):
+        count(7 * len(chunk_lines(chunk)), row_recv.at[chunk]).wait_recv()
+        for t, n in chunk_lines(chunk):
             at = (t * 4 + n) * 2
             w = jnp.concatenate([(want == linebags[at + h]).astype(F32) for h in range(2)], axis=1).astype(BF16)
             hi, lo = split2(agg[t, n].reshape(8 * CAP, E))
             part = dot(w, hi) + dot(w, lo)
             if t or n:
                 sums[t * 4 + n] = part
-                sum_copy(t, n).start()
+                sum_copy(chunk, t, n).start()
             else:
                 parts[0] = part
 
-    order = (2, 1, 3, 0)
-    for t in order:
+    push_early(ORDER[:EARLY])
+    for t in ORDER[EARLY:]:
         push(t)
     all_bags.wait_recv()
-    for t in order:
+    for t in ORDER:
         pool(t)
 
     total = jnp.zeros((BAGS, E), F32)
-    for t in order:
-        sums_of(t).wait_recv()
-        for n in range(4):
+    for chunk in ORDER:
+        lines = chunk_lines(chunk)
+        sums_of(len(lines) - (chunk == 0), chunk).wait_recv()
+        for t, n in lines:
             total = total + parts[t * 4 + n]
 
     feats = [dense] + [total[t * 16:(t + 1) * 16] for t in range(NT)]
@@ -261,9 +310,12 @@
     hidden_out[...] = jnp.maximum(hidden, 0.0)
 
     first.wait_send()
-    second.wait_send()
+    pltpu.make_async_remote_copy(
+        src_ref=passing.at[pl.ds(1, 15)], dst_ref=passing.at[pl.ds(1, 15)], send_sem=ids_send.at[1],
+        recv_sem=ids_recv.at[1], device_id=plane[1], device_id_type=MESH).wait_send()
+    relayed.wait_send()
     all_bags.wait_send()
-    count(28, row_send).wait_send()
+    count(112, row_send).wait_send()
     pltpu.make_async_remote_copy(
         src_ref=sums.at[pl.ds(1, 15)], dst_ref=parts.at[pl.ds(1, 15)], send_sem=sum_send, recv_sem=sum_recv.at[0],
         device_id=line[1], device_id_type=MESH).wait_send()
@@ -303,18 +355,19 @@
             pltpu.VMEM((16, 8, 1, CAP), I32),
             pltpu.SMEM((NDEV, 1, CAP), I32),
             pltpu.VMEM((32, 1, NDEV), I32),
+            pltpu.VMEM((18, 1, NDEV), I32),
             pltpu.VMEM((32, 1, NDEV), I32),
-            pltpu.VMEM((32, 4, CAP, E), F32),
+            pltpu.VMEM((NDEV, CAP, E), F32),
             pltpu.VMEM((4, 4, 4, 2, CAP, E), F32),
             pltpu.VMEM((16, BAGS, E), F32),
             pltpu.VMEM((16, BAGS, E), F32),
             pltpu.SemaphoreType.DMA((6,)),
             pltpu.SemaphoreType.DMA((TAB_PARTS,)),
             pltpu.SemaphoreType.DMA((2,)),
+            pltpu.SemaphoreType.DMA((16,)),
+            pltpu.SemaphoreType.DMA,
             pltpu.SemaphoreType.DMA((2,)),
-            pltpu.SemaphoreType.DMA,
-            pltpu.SemaphoreType.DMA,
-            pltpu.SemaphoreType.DMA,
+            pltpu.SemaphoreType.DMA((2,)),
             pltpu.SemaphoreType.DMA,
             pltpu.SemaphoreType.DMA((4,)),
             pltpu.SemaphoreType.DMA,

time: 34.8 us -> 33.4 us (0.960)
  Pallas kernels: 34 us -> 32.5 us
    pallas_call x1, Pallas kernels: 33.4 us -> 31.9 us  [shards(): pl.pallas_call(kernel, out_shape=outs, in_specs=[hbm] * 7, out_specs=(vme...]
where the time goes in v6:
time: 33.4 us; the launch traced here: 33.2 us
  Pallas kernels  32.5 us (97%)
  between operations  0.64 us (2%)
    pallas_call x1, Pallas kernels, shards(): pl.pallas_call(kernel, out_shape=outs, in_specs=[hbm] * 7, out_specs=(vme...  31.9 us

profile of v6, /device:TPU:0, one launch (start us, length us, event | category | flops | bytes accessed | tf_op | source)
XLA Modules:
  0.0 33.2 jit_solution(8641888741836578091)
XLA Ops:
  0.6 31.9 %shard_map.86 = (f32[16,4,128]{2,1,0:T(4,128)S(1)}, f32[16,1024]{1,0:T(8,128)S(1)}) custom-call(s32[16,128]{1,0:T(8,128)} %idx_hbm.1, s32[4,16]{1,0:T(4,128)} %bitcast.5, f32[32768,128]{1,0:T(8,128)} %bitcast.3, f32[16,128]{1,0:T(8,128)} %dense_hbm.1, f32[128,1024]{1,0:T(8,128)} %wd_hbm.1, f32[10,1024]{1,0:T(8,128)} %wp_hbm.1, f32[1,1024]{1,0:T(1,128)} %bitcast.4), custom_call_target="tpu_custom_call" | custom-call | tf_op jit(solution)/shard_map/pallas_call | solution.py:338
  32.5 0.7 %shard_map.87 = (f32[16,4,128]{2,1,0:T(4,128)}, f32[16,1024]{1,0:T(8,128)}) custom-call(f32[16,4,128]{2,1,0:T(4,128)S(1)} %get-tuple-element.4.pooled, f32[16,1024]{1,0:T(8,128)S(1)} %get-tuple-element.5.hidden), custom_call_target="tpu_custom_call" | custom-call | tf_op jit(solution)/shard_map/pallas_call | solution.py:381
